TPU v7x, 128 devices: a whole 4x4x4 slice. The times are simulated.
128 devices in a mesh: group: 8 (over z, x_hi), ep: 16 (over x_lo, y, core).
Axes of the slice: x: 4 (x_hi: 2, x_lo: 2; x = x_hi * 2 + x_lo), y: 4, z: 4, core: 2. Of those that a mesh axis runs over, the one named last changes fastest.
Arguments:
- tokens: bfloat16 [16384, 7168], P(('group', 'ep')), may hold values from -6 to 6
- expert_ids: int32 [16384, 4], P(('group', 'ep')), may hold values from 0 to 63, all different within a row; in each aligned block of 128 rows (0 to 127, 128 to 255, ...) at most 10 rows name the same one
- route_score: float32 [16384, 4], P(('group', 'ep')), may hold values from 0.1 to 1
- gate_weight: bfloat16 [128, 7168, 512], P(('group', 'ep')), may hold values from -0.0625 to 0.0625
- up_weight: bfloat16 [128, 7168, 512], P(('group', 'ep')), may hold values from -0.0625 to 0.0625
- down_weight: bfloat16 [128, 512, 7168], P(('group', 'ep')), may hold values from -0.1875 to 0.1875
Outputs:
- mixed: bfloat16 [16384, 7168], P(('group', 'ep'))
Inputs may be any that keep to these rules, and one draw needn't show every extreme that they name: `expert_ids`: among the 128 tokens of one device no expert is named by more than 10 of them, a bound that some block reaches; a token names 4 different experts.
All inputs are finite; a program needn't handle non-finite values.
Results may differ from a plain program's by a relative error of at most 0.0065.
Values may be sent and summed in bfloat16 or wider, within the bound.
A program may use at most 192 MiB of HBM per device.

v0:
```python
import jax
import jax.numpy as jnp
from jax import lax
from jax.sharding import PartitionSpec as P


def partner(value, axis, stride):
    return lax.ppermute(value, axis, [(i, i ^ 1 << stride) for i in range(lax.axis_size(axis))])


def split_up(value, dim, peers):
    before, after = (value.shape[:dim], value.shape[dim + 1 :])
    return jnp.moveaxis(value.reshape(*before, peers, -1, *after), dim, 0)


def piece_ends(length, count):
    unit = 8 if length >= 8 * count else 1
    return [length // unit * k // count * unit for k in range(1, count)]


def laid_out(pieces, dim):
    shape = list(pieces.shape[1:])
    shape[dim] *= pieces.shape[0]
    return jnp.moveaxis(pieces, 0, dim).reshape(shape)


def exchange_in_pieces(value, axis, pieces, split_dim, concat_dim):
    blocks = split_up(value, split_dim, lax.axis_size(axis))
    split_at = max(range(1, max(2, blocks.ndim - 1)), key=lambda d: blocks.shape[d])
    outs = []
    for slab in jnp.split(blocks, piece_ends(blocks.shape[split_at], pieces), axis=split_at):
        if slab.size:
            outs.append(lax.all_to_all(slab, axis, split_axis=0, concat_axis=0, tiled=True))
    return laid_out(jnp.concatenate(outs, axis=split_at), concat_dim)


def expert_half(incoming, gate_weight, up_weight, down_weight):
    flat_rows = incoming.reshape(-1, incoming.shape[-1])
    gate_out = jnp.dot(flat_rows, gate_weight[0], preferred_element_type=jnp.float32)
    up_out = jnp.dot(flat_rows, up_weight[0], preferred_element_type=jnp.float32)
    hidden = (jax.nn.silu(gate_out) * up_out).astype(jnp.bfloat16)
    result = jnp.dot(hidden, down_weight[0], preferred_element_type=jnp.float32).astype(
        jnp.bfloat16
    )
    return result.reshape(incoming.shape)


def deliver(buffer):
    return lax.all_to_all(buffer, ("group", "ep"), split_axis=0, concat_axis=0, tiled=True)


def add_pair(first, second):
    return (first.astype(jnp.float32) + second.astype(jnp.float32)).astype(jnp.bfloat16)


def shards(tokens, expert_ids, route_score, gate_weight, up_weight, down_weight):
    tok_rows, model_width = tokens.shape
    choose = expert_ids.shape[1]
    devices = lax.axis_size("group") * lax.axis_size("ep")
    experts = devices // 2
    capacity = 2 * ((5 * tok_rows * choose + 8 * experts - 1) // (8 * experts))
    half_slots = capacity // 2
    weight = 2.5 * route_score / jnp.sum(route_score, axis=1, keepdims=True)
    flat_ids = expert_ids.reshape(-1)
    onehot = (flat_ids[:, None] == jnp.arange(experts, dtype=jnp.int32)[None, :]).astype(jnp.int32)
    slot_of = jnp.sum(onehot * jnp.cumsum(onehot, axis=0), axis=1) - 1
    position = flat_ids * capacity + slot_of
    token_flat = jnp.arange(tok_rows * choose, dtype=jnp.int32) // choose
    source_tok = jnp.zeros((experts * capacity,), jnp.int32).at[position].set(token_flat)
    outgoing = tokens[source_tok].reshape(experts, capacity, model_width)
    doubled = jnp.broadcast_to(outgoing[:, None], (experts, 2, capacity, model_width))
    arrived = deliver(doubled.reshape(devices, capacity, model_width))
    partial_value = expert_half(arrived, gate_weight, up_weight, down_weight)
    side = lax.axis_index("ep") % 2
    kept = lax.dynamic_slice_in_dim(partial_value, side * half_slots, half_slots, 1)
    given = lax.dynamic_slice_in_dim(partial_value, (1 - side) * half_slots, half_slots, 1)
    received = partner(given, "ep", 0)
    combined = add_pair(kept, received)
    returned = exchange_in_pieces(combined, ("group", "ep"), 2, 0, 0)
    summed = returned.reshape(experts, capacity, model_width)
    summed = summed.reshape(experts * capacity, model_width)
    picked = summed[position].reshape(tok_rows, choose, model_width).astype(jnp.float32)
    return jnp.sum(weight[:, :, None] * picked, axis=1).astype(jnp.bfloat16)


def solution(mesh):
    in_specs = (
        P(("group", "ep"), None),
        P(("group", "ep"), None),
        P(("group", "ep"), None),
        P(("group", "ep"), None, None),
        P(("group", "ep"), None, None),
        P(("group", "ep"), None, None),
    )
    out_specs = P(("group", "ep"), None)
    return jax.shard_map(shards, mesh=mesh, in_specs=in_specs, out_specs=out_specs, check_vma=False)
```

profile of v0, /device:TPU:2, one launch (start us, length us, event | category | flops | bytes accessed | tf_op | source)
XLA Modules:
  0.0 860.5 jit_solution(7637270750143227687)
XLA Ops:
  6.2 8.8 %gather_fusion = bf16[640,7168]{1,0:T(8,128)(2,1)} fusion(bf16[128,7168]{1,0:T(8,128)(2,1)S(1)} %copy-done, s32[1024]{0:T(1024)S(1)} %pad_clamp_fusion.1), kind=kCustom, calls=%fused_computation | custom fusion | bytes 18352640 | tf_op jit(solution)/shard_map/gather | solution.py:70
  15.0 14.4 %broadcast_in_dim.7 = bf16[64,10,7168]{2,1,0:T(8,128)(2,1)} reshape(bf16[640,7168]{1,0:T(8,128)(2,1)} %gather_fusion) | data formatting | bytes 18350080 | tf_op jit(solution)/shard_map/broadcast_in_dim | solution.py:71
  29.5 14.0 %broadcast_in_dim.8 = bf16[64,2,10,7168]{3,2,1,0:T(8,128)(2,1)} broadcast(bf16[64,10,7168]{2,1,0:T(8,128)(2,1)} %broadcast_in_dim.7), dimensions={0,2,3} | broadcast | bytes 27525120 | tf_op jit(solution)/shard_map/broadcast_in_dim | solution.py:71
  43.4 10.9 %all-to-all-start = ((bf16[128,10,7168]{2,1,0:T(8,128)(2,1)}), bf16[128,10,7168]{2,1,0:T(8,128)(2,1)}, u32[]{:S(2)}, u32[]{:S(2)}) async-start(bf16[128,10,7168]{2,1,0:T(8,128)(2,1)} %bitcast.40), calls=%async_computation | async-start | bytes 58720256 | tf_op jit(solution)/shard_map/all_to_all | solution.py:49
  54.4 421.0 %all-to-all-done = bf16[128,10,7168]{2,1,0:T(8,128)(2,1)} async-done(((bf16[128,10,7168]{2,1,0:T(8,128)(2,1)}), bf16[128,10,7168]{2,1,0:T(8,128)(2,1)}, u32[]{:S(2)}, u32[]{:S(2)}) %all-to-all-start) | async-done | bytes 18350112 | tf_op jit(solution)/shard_map/all_to_all | solution.py:49
  475.4 28.2 %reshape.71 = bf16[1280,7168]{1,0:T(8,128)(2,1)} reshape(bf16[128,10,7168]{2,1,0:T(8,128)(2,1)} %all-to-all-done) | data formatting | bytes 36700160 | tf_op jit(solution)/shard_map/reshape | solution.py:38
  503.6 16.7 %fusion.4 = f32[1280,512]{1,0:T(8,128)} fusion(bf16[1280,7168]{1,0:T(8,128)(2,1)} %reshape.71, bf16[1,7168,512]{2,1,0:T(8,128)(2,1)} %param.9), kind=kOutput, calls=%fused_computation.12 | convolution fusion | flops 9395240960 | bytes 28311552 | tf_op jit(solution)/shard_map/dot_general | solution.py:39
  520.3 13.3 %fusion.9 = bf16[1280,512]{1,0:T(8,128)(2,1)S(1)} fusion(bf16[1280,7168]{1,0:T(8,128)(2,1)S(1)} %copy-done.3, bf16[1,7168,512]{2,1,0:T(8,128)(2,1)} %param.10, f32[1280,512]{1,0:T(8,128)} %fusion.4), kind=kOutput, calls=%fused_computation.16 | convolution fusion | flops 9399173120 | bytes 29622272 | tf_op jit(solution)/shard_map/dot_general | solution.py:40
  533.6 15.8 %convolution_convert_fusion = bf16[1280,7168]{1,0:T(8,128)(2,1)} fusion(bf16[1280,512]{1,0:T(8,128)(2,1)S(1)} %fusion.9, bf16[1,512,7168]{2,1,0:T(8,128)(2,1)} %param.11), kind=kOutput, calls=%fused_computation.4 | convolution fusion | flops 9404416000 | bytes 27000832 | tf_op jit(solution)/shard_map/dot_general | solution.py:42
  549.5 27.7 %reshape.72 = bf16[128,10,7168]{2,1,0:T(8,128)(2,1)} reshape(bf16[1280,7168]{1,0:T(8,128)(2,1)} %convolution_convert_fusion) | data formatting | bytes 36700160 | tf_op jit(solution)/shard_map/reshape | solution.py:45
  577.2 13.2 %constant_dynamic-slice_fusion = bf16[128,5,7168]{2,1,0:T(8,128)(2,1)S(1)} fusion(bf16[128,10,7168]{2,1,0:T(8,128)(2,1)} %reshape.72, s32[]{:T(128)S(6)} %select_n.37), kind=kLoop, calls=%fused_computation.41 | loop fusion | bytes 18350084 | tf_op jit(solution)/shard_map/dynamic_slice | solution.py:76
  590.4 7.8 copy.18
  598.2 14.6 %collective-permute-done = bf16[128,5,7168]{2,0,1:T(8,128)(2,1)} collective-permute-done((bf16[128,5,7168]{2,0,1:T(8,128)(2,1)}, bf16[128,5,7168]{2,0,1:T(8,128)(2,1)}, u32[]{:S(2)}, u32[]{:S(2)}) %collective-permute-start) | collective-permute-done | bytes 9175072 | tf_op jit(solution)/shard_map/ppermute | solution.py:8
  612.8 18.0 %fusion = bf16[128,1,5,7168]{3,2,0,1:T(8,128)(2,1)S(1)} fusion(bf16[128,5,7168]{2,0,1:T(8,128)(2,1)} %collective-permute-done, bf16[128,10,7168]{2,1,0:T(8,128)(2,1)} %reshape.72, s32[]{:T(128)S(6)} %select_n.36), kind=kLoop, calls=%fused_computation.5 | loop fusion | flops 18350080 | bytes 27525124 | tf_op jit(solution)/shard_map/reshape | solution.py:13
  640.3 8.0 all-to-all-start.1
  648.4 9.7 %slice_bitcast_fusion = bf16[128,1,3,7168]{3,2,1,0:T(4,128)(2,1)} fusion(bf16[128,1,5,7168]{3,2,0,1:T(8,128)(2,1)} %copy-done.2), kind=kLoop, calls=%fused_computation.8 | loop fusion | bytes 11010048 | tf_op jit(solution)/shard_map/split | solution.py:31
  658.2 36.8 %all-to-all-done.1 = bf16[128,1,2,7168]{3,2,1,0:T(2,128)(2,1)} async-done(((bf16[128,1,2,7168]{3,2,1,0:T(2,128)(2,1)}), bf16[128,1,2,7168]{3,2,1,0:T(2,128)(2,1)}, u32[]{:S(2)}, u32[]{:S(2)}) %all-to-all-start.1) | async-done | bytes 3670048 | tf_op jit(solution)/shard_map/all_to_all | solution.py:33
  695.0 6.1 all-to-all-start.2
  701.2 87.0 %all-to-all-done.2 = bf16[128,1,3,7168]{3,2,1,0:T(4,128)(2,1)} async-done(((bf16[128,1,3,7168]{3,2,1,0:T(4,128)(2,1)}), bf16[128,1,3,7168]{3,2,1,0:T(4,128)(2,1)}, u32[]{:S(2)}, u32[]{:S(2)}) %all-to-all-start.2) | async-done | bytes 5505056 | tf_op jit(solution)/shard_map/all_to_all | solution.py:33
  788.2 11.1 %pad_maximum_fusion = bf16[128,1,5,7168]{3,2,1,0:T(8,128)(2,1)} fusion(bf16[128,1,3,7168]{3,2,1,0:T(4,128)(2,1)} %all-to-all-done.2, bf16[128,1,2,7168]{3,2,1,0:T(2,128)(2,1)} %all-to-all-done.1), kind=kLoop, calls=%fused_computation.6 | loop fusion | flops 18350080 | bytes 18350080 | tf_op jit(solution)/shard_map/concatenate | solution.py:34
  799.3 15.1 %reshape_reshape_reshape.3 = bf16[640,7168]{1,0:T(8,128)(2,1)} reshape(bf16[128,1,5,7168]{3,2,1,0:T(8,128)(2,1)} %pad_maximum_fusion) | data formatting | bytes 18350080 | tf_op jit(solution)/shard_map/reshape;reshape;reshape | solution.py:81
  814.3 18.7 %gather_fusion.1 = bf16[512,7168]{1,0:T(8,128)(2,1)} fusion(bf16[640,7168]{1,0:T(8,128)(2,1)} %reshape_reshape_reshape.3, s32[1024]{0:T(1024)S(1)} %pad_clamp_fusion), kind=kCustom, calls=%fused_computation.1 | custom fusion | bytes 14682112 | tf_op jit(solution)/shard_map/gather | solution.py:82
  833.0 14.1 %reshape.74 = f32[128,4,7168]{2,1,0:T(4,128)} reshape(bf16[512,7168]{1,0:T(8,128)(2,1)} %gather_fusion.1) | data formatting | bytes 22020096 | tf_op jit(solution)/shard_map/convert_element_type | solution.py:82
  847.1 13.5 %multiply_reduce_fusion = bf16[128,7168]{1,0:T(8,128)(2,1)} fusion(f32[128,4,7168]{2,1,0:T(4,128)} %reshape.74, f32[128,4]{1,0:T(8,128)S(1)} %copy.13), kind=kLoop, calls=%fused_computation.7 | loop fusion | flops 6422528 | bytes 16517120 | tf_op jit(solution)/shard_map/reduce_sum | solution.py:83
  (38 shorter events, 15.8 us)
Async XLA Ops:
  0.0 6.2 copy-start
  3.7 11.3 %copy-start.4 = (s32[512,1]{0,1:T(1,128)}, s32[512,1]{0,1:T(1,128)S(1)}, u32[]{:S(2)}) copy-start(s32[512,1]{0,1:T(1,128)S(1)} %compare_select_fusion) | copy-start | bytes 6148
  43.4 431.9 %all-to-all-start = ((bf16[128,10,7168]{2,1,0:T(8,128)(2,1)}), bf16[128,10,7168]{2,1,0:T(8,128)(2,1)}, u32[]{:S(2)}, u32[]{:S(2)}) async-start(bf16[128,10,7168]{2,1,0:T(8,128)(2,1)} %bitcast.40), calls=%async_computation | async-start | bytes 58720256 | tf_op jit(solution)/shard_map/all_to_all | solution.py:49
  503.6 16.7 %copy-start.3 = (bf16[1280,7168]{1,0:T(8,128)(2,1)S(1)}, bf16[1280,7168]{1,0:T(8,128)(2,1)}, u32[]{:S(2)}) copy-start(bf16[1280,7168]{1,0:T(8,128)(2,1)} %reshape.71) | copy-start | bytes 55050244
  598.2 14.6 %collective-permute-start = (bf16[128,5,7168]{2,0,1:T(8,128)(2,1)}, bf16[128,5,7168]{2,0,1:T(8,128)(2,1)}, u32[]{:S(2)}, u32[]{:S(2)}) collective-permute-start(bf16[128,5,7168]{2,0,1:T(8,128)(2,1)} %copy.18), channel_id=1, source_target_pairs={{0,1},{1,0},{2,3},{3,2},{4,5},{5,4},{6,7},{7,6},{8,9},{9,8},{10,11... | collective-permute-start | bytes 27525128 | tf_op jit(solution)/shard_map/ppermute | solution.py:8
  630.8 5.2 copy-start.2
  640.3 54.6 %all-to-all-start.1 = ((bf16[128,1,2,7168]{3,2,1,0:T(2,128)(2,1)}), bf16[128,1,2,7168]{3,2,1,0:T(2,128)(2,1)}, u32[]{:S(2)}, u32[]{:S(2)}) async-start(bf16[128,1,2,7168]{3,2,1,0:T(2,128)(2,1)} %slice_bitcast_fusion.1), calls=%async_computation.1 | async-start | bytes 7340032 | tf_op jit(solution)/shard_map/all_to_all | solution.py:33
  658.1 42.9 %copy-start.6 = (f32[128,4]{0,1:T(4,128)S(1)}, f32[128,4]{0,1:T(4,128)}, u32[]{:S(2)}) copy-start(f32[128,4]{0,1:T(4,128)} %param.8) | copy-start | bytes 6148
  658.2 43.0 %copy-start.5 = (s32[512,1]{0,1:T(1,128)S(1)}, s32[512,1]{0,1:T(1,128)}, u32[]{:S(2)}) copy-start(s32[512,1]{0,1:T(1,128)} %copy-done.4) | copy-start | bytes 6148
  695.0 93.2 %all-to-all-start.2 = ((bf16[128,1,3,7168]{3,2,1,0:T(4,128)(2,1)}), bf16[128,1,3,7168]{3,2,1,0:T(4,128)(2,1)}, u32[]{:S(2)}, u32[]{:S(2)}) async-start(bf16[128,1,3,7168]{3,2,1,0:T(4,128)(2,1)} %slice_bitcast_fusion), calls=%async_computation.2 | async-start | bytes 14680064 | tf_op jit(solution)/shard_map/all_to_all | solution.py:33
  833.0 27.5 %copy-start.1 = (bf16[128,7168]{1,0:T(8,128)(2,1)S(1)}, bf16[128,7168]{1,0:T(8,128)(2,1)}, u32[]{:S(2)}) copy-start(bf16[128,7168]{1,0:T(8,128)(2,1)} %param.6) | copy-start | bytes 5505028
where the time goes:
time: 864 us; the launch traced here: 861 us
  waiting for transfers between devices  559 us (65%)
  local copies, waits for them, and re-layouts  185 us (21%)
  matrix products  45.9 us (5%)
  other arithmetic  44.7 us (5%)
  starting transfers between devices  25.1 us (3%)
    all_to_all x1, waiting for transfers between devices, deliver(): lax.all_to_all(buffer, ('group', 'ep'), split_axis=0, concat_axis=0, tile...  421 us
    all_to_all x2, waiting for transfers between devices, exchange_in_pieces(): lax.all_to_all(slab, axis, split_axis=0, concat_axis=0, tiled=True)  124 us
    broadcast_in_dim x2, local copies, waits for them, and re-layouts, shards(): jnp.broadcast_to(outgoing[:, None], (experts, 2, capacity, model_width))  28.4 us
    reshape x1, local copies, waits for them, and re-layouts, expert_half(): flat_rows = incoming.reshape(-1, incoming.shape[-1])  28.2 us
    reshape x1, local copies, waits for them, and re-layouts, expert_half(): return result.reshape(incoming.shape)  27.7 us
    dynamic_slice x2, local copies, waits for them, and re-layouts, shards(): lax.dynamic_slice_in_dim(partial_value, (1 - side) * half_slots, half_slo...  21 us
    gather x1, local copies, waits for them, and re-layouts, shards(): summed[position].reshape(tok_rows, choose, model_width).astype(jnp.float32)  18.7 us
    reshape x1, other arithmetic, split_up(): return jnp.moveaxis(value.reshape(*before, peers, -1, *after), dim, 0)  18 us
  transfers between devices with their start and end apart: 4, of which 4 were waited for; matrix products, arithmetic and copies ran while one was open for 1% of the time, Pallas kernels for 0%

commit v1 on v0

v1 whole, which is shorter than its diff:
```python
import functools

import jax
import jax.numpy as jnp
from jax import lax
from jax.experimental import pallas as pl
from jax.experimental.pallas import tpu as pltpu
from jax.sharding import PartitionSpec as P

D = 7168
FFH = 512
TOPK = 4
TOK = 128
EXPERTS = 64
HEAD = 8
QUARTER = D // 4
CHUNKS = 4
PER = EXPERTS // CHUNKS
ROWS = PER * HEAD + PER * 2
MESH = pl.DeviceIdType.MESH
F32 = jnp.float32
BF16 = jnp.bfloat16


def iota(shape, dim):
    return lax.broadcasted_iota(jnp.int32, shape, dim)


def prep_kernel(tokens, ids, score, head, tail, w_head, w_tail):
    weight = 2.5 * score[...] / jnp.sum(score[...], axis=1, keepdims=True)
    expert = iota((TOK, EXPERTS), 1)
    named = [(ids[:, k : k + 1] == expert).astype(F32) for k in range(TOPK)]
    before = (iota((TOK, TOK), 1) < iota((TOK, TOK), 0)).astype(BF16)
    counts = jnp.dot(before, sum(named).astype(BF16), preferred_element_type=F32)
    column = iota((TOK, EXPERTS * HEAD), 1)
    pick_head = jnp.zeros((TOK, EXPERTS * HEAD), F32)
    pick_tail = jnp.zeros((TOK, EXPERTS * HEAD), F32)
    wt_head = jnp.zeros((TOK, EXPERTS * HEAD), F32)
    wt_tail = jnp.zeros((TOK, EXPERTS * HEAD), F32)
    for k in range(TOPK):
        slot = jnp.sum(counts * named[k], axis=1, keepdims=True).astype(jnp.int32)
        own = (column // HEAD) == ids[:, k : k + 1]
        hit_head = jnp.where(own & (column % HEAD == slot), 1.0, 0.0)
        hit_tail = jnp.where(own & (column % 2 + HEAD == slot), 1.0, 0.0)
        pick_head += hit_head
        pick_tail += hit_tail
        wt_head += hit_head * weight[:, k : k + 1]
        wt_tail += hit_tail * weight[:, k : k + 1]
    w_head[...] = wt_head.astype(BF16)
    w_tail[...] = wt_tail.astype(BF16)
    contract = (((0,), (0,)), ((), ()))
    rows = pick_head.T.astype(BF16)
    for n in range(4):
        at = slice(n * QUARTER, (n + 1) * QUARTER)
        head[:, at] = jnp.dot(rows, tokens[:, at], preferred_element_type=F32).astype(BF16)
    turned = pick_tail.T
    quarter = (iota((EXPERTS * HEAD, TOK), 0) % HEAD) // 2
    total = jnp.zeros((EXPERTS * HEAD, QUARTER), F32)
    for q in range(4):
        part = jnp.where(quarter == q, turned, 0.0).astype(BF16)
        at = slice(q * QUARTER, (q + 1) * QUARTER)
        total += jnp.dot(part, tokens[:, at], preferred_element_type=F32)
    tail[...] = total.astype(BF16)


def prep(tokens, ids, score):
    wide = EXPERTS * HEAD
    return pl.pallas_call(
        prep_kernel,
        out_shape=(
            jax.ShapeDtypeStruct((wide, D), BF16),
            jax.ShapeDtypeStruct((wide, QUARTER), BF16),
            jax.ShapeDtypeStruct((TOK, wide), BF16),
            jax.ShapeDtypeStruct((TOK, wide), BF16),
        ),
        compiler_params=pltpu.CompilerParams(vmem_limit_bytes=48 * 2**20),
    )(tokens, ids, score)


def offset(i):
    i0, i1, i2 = i % 4, (i // 4) % 4, i // 16
    return i0, (i0 + i1) % 4, (i0 + i1 + i2) % 4


def device(z, x, y, c):
    return (z * 2 + x // 2, ((x % 2) * 4 + y) * 2 + c)


def moe_kernel(
    head, tail, wg, wu, wd, yh, yt,
    xs, ts, wgv, wuv, wdv, hid,
    own_sem, give_sem, take_sem,
    out_h, out_t, in_h, in_t, ret_h, ret_t, back_h, back_t,
):
    group, ep = lax.axis_index("group"), lax.axis_index("ep")
    z, x, y, c = group // 2, (group % 2) * 2 + ep // 8, (ep // 2) % 4, ep % 2
    me = z * 16 + x * 4 + y

    def ahead(i):
        dz, dx, dy = offset(i)
        tz, tx, ty = (z + dz) % 4, (x + dx) % 4, (y + dy) % 4
        return tz * 16 + tx * 4 + ty, device(tz, tx, ty, c)

    def behind(i):
        dz, dx, dy = offset(i)
        return device((z + 4 - dz) % 4, (x + 4 - dx) % 4, (y + 4 - dy) % 4, c)

    def block(i):
        return pl.ds(pl.multiple_of(i * HEAD, HEAD), HEAD)

    barrier = pltpu.get_barrier_semaphore()

    def greet(i, carry):
        pl.semaphore_signal(barrier, inc=1, device_id=ahead(i)[1], device_id_type=MESH)
        return carry

    lax.fori_loop(1, EXPERTS, greet, 0)
    partner = device(z, x, y, 1 - c)
    pl.semaphore_signal(barrier, inc=1, device_id=partner, device_id_type=MESH)
    pl.semaphore_wait(barrier, EXPERTS)

    pltpu.make_async_copy(head.at[block(me)], xs.at[0, block(0)], in_h.at[0]).start()
    pltpu.make_async_copy(tail.at[block(me)], ts.at[0, block(0)], in_t.at[0]).start()

    def dispatch(i, carry):
        chip, dev = ahead(i)
        pltpu.make_async_remote_copy(
            src_ref=head.at[block(chip)], dst_ref=xs.at[i // PER, block(i % PER)],
            send_sem=out_h, recv_sem=in_h.at[i // PER], device_id=dev, device_id_type=MESH,
        ).start()
        pltpu.make_async_remote_copy(
            src_ref=tail.at[block(chip)], dst_ref=ts.at[i // PER, block(i % PER)],
            send_sem=out_t, recv_sem=in_t.at[i // PER], device_id=dev, device_id_type=MESH,
        ).start()
        return carry

    lax.fori_loop(1, EXPERTS, dispatch, 0)

    own, give = [], []
    for n, (source, target) in enumerate(((wg, wgv), (wu, wuv), (wd, wdv))):
        own.append(pltpu.make_async_copy(source.at[0], target.at[0], own_sem.at[n]))
        give.append(pltpu.make_async_remote_copy(
            src_ref=source.at[0], dst_ref=target.at[1],
            send_sem=give_sem.at[n], recv_sem=take_sem.at[n],
            device_id=partner, device_id_type=MESH,
        ))
        own[-1].start()
        give[-1].start()

    a = iota((PER * HEAD, PER * HEAD), 0)
    b = iota((PER * HEAD, PER * HEAD), 1)
    spread = (b == (a % 32) // 2 * HEAD + a // 32 * 2 + a % 2).astype(BF16)
    gather = (a == (b % 32) // 2 * HEAD + b // 32 * 2 + b % 2).astype(BF16)
    top = PER * HEAD

    def step(chunk, carry):
        pltpu.make_async_copy(
            xs.at[chunk, pl.ds(0, top)], xs.at[chunk, pl.ds(0, top)], in_h.at[chunk]
        ).wait()
        pltpu.make_async_copy(ts.at[chunk], ts.at[chunk], in_t.at[chunk]).wait()

        @pl.when(chunk == 0)
        def _():
            for n in range(3):
                own[n].wait()
                give[n].wait_recv()

        moved = jnp.dot(spread, ts[chunk], preferred_element_type=F32).astype(BF16)
        for q in range(4):
            xs[chunk, top:, q * QUARTER : (q + 1) * QUARTER] = moved[q * 32 : (q + 1) * 32]

        def up(n, carry):
            at = pl.ds(pl.multiple_of((n % 2) * 256, 256), 256)
            gate = jnp.zeros((ROWS, 256), F32)
            lift = jnp.zeros((ROWS, 256), F32)
            for k in range(7):
                rows = slice(k * 1024, (k + 1) * 1024)
                left = xs[chunk, :, rows]
                gate += jnp.dot(left, wgv[n // 2, rows, at], preferred_element_type=F32)
                lift += jnp.dot(left, wuv[n // 2, rows, at], preferred_element_type=F32)
            hid[n] = (gate / (1.0 + jnp.exp(-gate)) * lift).astype(BF16)
            return carry

        lax.fori_loop(0, 4, up, 0)

        def down(n, carry):
            at = pl.ds(pl.multiple_of(n * 512, 512), 512)
            total = jnp.zeros((ROWS, 512), F32)
            for k in range(4):
                total += jnp.dot(
                    hid[k], wdv[k // 2, (k % 2) * 256 : (k % 2) * 256 + 256, at],
                    preferred_element_type=F32,
                )
            xs[chunk, :, at] = total.astype(BF16)
            return carry

        lax.fori_loop(0, 14, down, 0)

        stacked = jnp.concatenate(
            [xs[chunk, top:, q * QUARTER : (q + 1) * QUARTER] for q in range(4)], axis=0
        )
        ts[chunk] = jnp.dot(gather, stacked, preferred_element_type=F32).astype(BF16)

        def back(r, carry):
            i = chunk * PER + r

            @pl.when(i == 0)
            def _():
                pltpu.make_async_copy(xs.at[0, block(0)], yh.at[block(me)], back_h).start()
                pltpu.make_async_copy(ts.at[0, block(0)], yt.at[block(me)], back_t).start()

            @pl.when(i > 0)
            def _():
                dev = behind(i)
                pltpu.make_async_remote_copy(
                    src_ref=xs.at[chunk, block(r)], dst_ref=yh.at[block(me)],
                    send_sem=ret_h, recv_sem=back_h, device_id=dev, device_id_type=MESH,
                ).start()
                pltpu.make_async_remote_copy(
                    src_ref=ts.at[chunk, block(r)], dst_ref=yt.at[block(me)],
                    send_sem=ret_t, recv_sem=back_t, device_id=dev, device_id_type=MESH,
                ).start()

            return carry

        lax.fori_loop(0, PER, back, 0)
        return carry

    lax.fori_loop(0, CHUNKS, step, 0)
    for n in range(3):
        give[n].wait_send()
    most = pl.ds(0, (EXPERTS - 1) * HEAD)
    for sem, ref in ((out_h, yh.at[most]), (out_t, yt.at[most]), (ret_h, yh.at[most]),
                     (ret_t, yt.at[most]), (back_h, yh), (back_t, yt)):
        pltpu.make_async_copy(ref, ref, sem).wait()


def moe(head, tail, wg, wu, wd):
    anywhere = pl.BlockSpec(memory_space=pltpu.HBM)
    dma = pltpu.SemaphoreType.DMA
    return pl.pallas_call(
        moe_kernel,
        out_shape=(
            jax.ShapeDtypeStruct((EXPERTS * HEAD, D), BF16),
            jax.ShapeDtypeStruct((EXPERTS * HEAD, QUARTER), BF16),
        ),
        in_specs=[anywhere] * 5,
        out_specs=(anywhere, anywhere),
        scratch_shapes=[
            pltpu.VMEM((CHUNKS, ROWS, D), BF16),
            pltpu.VMEM((CHUNKS, PER * HEAD, QUARTER), BF16),
            pltpu.VMEM((2, D, FFH), BF16),
            pltpu.VMEM((2, D, FFH), BF16),
            pltpu.VMEM((2, FFH, D), BF16),
            pltpu.VMEM((4, ROWS, 256), BF16),
            dma((3,)), dma((3,)), dma((3,)),
            dma, dma, dma((CHUNKS,)), dma((CHUNKS,)), dma, dma, dma, dma,
        ],
        compiler_params=pltpu.CompilerParams(
            collective_id=0, has_side_effects=True, vmem_limit_bytes=67043328
        ),
    )(head, tail, wg, wu, wd)


def combine_kernel(w_head, w_tail, yh, yt, out):
    quarter = (iota((TOK, EXPERTS * HEAD), 1) % HEAD) // 2
    mine = jnp.where(quarter == pl.program_id(0), w_tail[...].astype(F32), 0.0).astype(BF16)
    total = jnp.dot(w_head[...], yh[...], preferred_element_type=F32)
    total += jnp.dot(mine, yt[...], preferred_element_type=F32)
    out[...] = total.astype(BF16)


def combine(w_head, w_tail, yh, yt):
    wide = EXPERTS * HEAD
    return pl.pallas_call(
        combine_kernel,
        grid=(4,),
        out_shape=jax.ShapeDtypeStruct((TOK, D), BF16),
        in_specs=[
            pl.BlockSpec((TOK, wide), lambda q: (0, 0)),
            pl.BlockSpec((TOK, wide), lambda q: (0, 0)),
            pl.BlockSpec((wide, QUARTER), lambda q: (0, q)),
            pl.BlockSpec((wide, QUARTER), lambda q: (0, 0)),
        ],
        out_specs=pl.BlockSpec((TOK, QUARTER), lambda q: (0, q)),
        compiler_params=pltpu.CompilerParams(vmem_limit_bytes=32 * 2**20),
    )(w_head, w_tail, yh, yt)


def shards(tokens, expert_ids, route_score, gate_weight, up_weight, down_weight):
    head, tail, w_head, w_tail = prep(tokens, expert_ids, route_score)
    yh, yt = moe(head, tail, gate_weight, up_weight, down_weight)
    return combine(w_head, w_tail, yh, yt)


def solution(mesh):
    tokens = P(("group", "ep"), None)
    weights = P(("group", "ep"), None, None)
    return jax.shard_map(
        shards, mesh=mesh, in_specs=(tokens,) * 3 + (weights,) * 3, out_specs=tokens,
        check_vma=False,
    )
```

time: 864 us -> 307 us (0.36)
  the two profiles are of different devices: /device:TPU:2 before, /device:TPU:98 now
where the time goes in v1:
time: 307 us
  Pallas kernels  295 us (96%)
  local copies, waits for them, and re-layouts  12 us (4%)
    pallas_call x1, Pallas kernels, moe(): pl.pallas_call(moe_kernel, out_shape=(jax.ShapeDtypeStruct((EXPERTS * HEA...  285 us
    unnamed x18, local copies, waits for them, and re-layouts  12 us

profile of v1, /device:TPU:98, one launch (start us, length us, event | category | flops | bytes accessed | tf_op | source)
XLA Modules:
  0.0 306.8 jit_solution(2006994833418841164)
XLA Ops:
  0.0 0.8 copy.7.ids
  0.8 0.8 copy.8.score
  1.6 0.0 copy-start.1
  1.6 1.5 copy-done.1
  3.1 5.9 %shard_map.64 = (bf16[512,7168]{1,0:T(8,128)(2,1)}, bf16[512,1792]{1,0:T(8,128)(2,1)S(1)}, bf16[128,512]{1,0:T(8,128)(2,1)S(1)}, bf16[128,512]{1,0:T(8,128)(2,1)S(1)}) custom-call(bf16[128,7168]{1,0:T(8,128)(2,1)S(1)} %copy-done.1, s32[128,4]{1,0:T(8,128)S(1)} %copy.7.ids, f32[128,4]{1,0:T(8,128)S(1)} %copy.8.score), custom_call_target="tpu_custom_call" | custom-call | tf_op jit(solution)/shard_map/pallas_call | solution.py:68
  9.0 0.0 copy-start.3
  9.0 1.2 copy-done.3
  10.2 0.0 copy-start.4
  10.2 0.7 copy-done.4
  10.9 0.0 copy-start.6
  10.9 0.6 copy-done.6
  11.5 285.0 %shard_map.65 = (bf16[512,7168]{1,0:T(8,128)(2,1)}, bf16[512,1792]{1,0:T(8,128)(2,1)}) custom-call(bf16[512,7168]{1,0:T(8,128)(2,1)} %get-tuple-element.13.head, bf16[512,1792]{1,0:T(8,128)(2,1)} %copy-done.3, bf16[1,7168,512]{2,1,0:T(8,128)(2,1)} %wg.1, bf16[1,7168,512]{2,1,0:T(8,128)(2,1)} %wu.1, bf16[1,512,7168]{2,1,0:T(8,128)(2,1)} %wd.1), custom_call_target="tpu_custom_call" | custom-call | tf_op jit(solution)/shard_map/pallas_call | solution.py:241
  296.5 0.0 copy-start
  296.5 3.1 %copy-done = bf16[512,7168]{1,0:T(8,128)(2,1)S(1)} copy-done((bf16[512,7168]{1,0:T(8,128)(2,1)S(1)}, bf16[512,7168]{1,0:T(8,128)(2,1)}, u32[]{:S(2)}) %copy-start) | copy-done | bytes 7340056
  299.6 0.0 copy-start.2
  299.6 1.5 copy-done.2
  301.1 0.0 copy-start.5
  301.1 0.9 copy-done.5
  302.0 0.0 copy-start.7
  302.0 0.9 copy-done.7
  302.9 3.9 %shard_map.66 = bf16[128,7168]{1,0:T(8,128)(2,1)} custom-call(bf16[128,512]{1,0:T(8,128)(2,1)S(1)} %copy-done.5, bf16[128,512]{1,0:T(8,128)(2,1)S(1)} %copy-done.7, bf16[512,7168]{1,0:T(8,128)(2,1)S(1)} %copy-done, bf16[512,1792]{1,0:T(8,128)(2,1)S(1)} %copy-done.2), custom_call_target="tpu_custom_call" | custom-call | tf_op jit(solution)/shard_map/pallas_call | solution.py:275
Async XLA Ops:
  1.6 1.5 copy-start.1
  9.0 1.2 copy-start.3
  10.2 0.7 copy-start.4
  10.9 0.6 copy-start.6
  296.5 3.1 %copy-start = (bf16[512,7168]{1,0:T(8,128)(2,1)S(1)}, bf16[512,7168]{1,0:T(8,128)(2,1)}, u32[]{:S(2)}) copy-start(bf16[512,7168]{1,0:T(8,128)(2,1)} %get-tuple-element.15.yh) | copy-start | bytes 22020100
  299.6 1.5 copy-start.2
  301.1 0.9 copy-start.5
  302.0 0.9 copy-start.7
